TPU v7x, 32 devices: a whole 2x2x4 slice. The times are simulated.
32 devices in a mesh: batch: 4 (over y, x), heads: 8 (over z, core).
Axes of the slice: x: 2, y: 2, z: 4, core: 2. Of those that a mesh axis runs over, the one named last changes fastest.
Arguments:
- draft_ids: int32 [192, 8], P('batch'), may hold values from 0 to 50279
- accepted: int32 [192], P('batch'), may hold values from 1 to 8
- embedding: bfloat16 [50280, 2560], P(None, 'heads'), may hold values from -6 to 6
- norm_gain: float32 [2, 2560], replicated, may hold values from 0.5 to 1.5
- w_zx: bfloat16 [2, 2560, 8, 128], P(None, None, 'heads'), may hold values from -0.125 to 0.125
- w_dt: bfloat16 [2, 2560, 8], P(None, None, 'heads'), may hold values from -0.125 to 0.125
- w_bc: bfloat16 [2, 2560, 256], P(None, None, 'heads'), may hold values from -0.125 to 0.125
- dt_bias: float32 [2, 8], P(None, 'heads'), may hold values from -4 to -1
- decay_rate: float32 [2, 8], P(None, 'heads'), may hold values from 1 to 16
- skip_weight: float32 [2, 8], P(None, 'heads'), may hold values from 0.5 to 1.5
- conv_x_w: bfloat16 [2, 4, 512], P(None, None, 'heads'), may hold values from -3 to 3
- conv_x_b: bfloat16 [2, 512], P(None, 'heads'), may hold values from -3 to 3
- conv_bc_w: bfloat16 [2, 4, 256], P(None, None, 'heads'), may hold values from -3 to 3
- conv_bc_b: bfloat16 [2, 256], P(None, 'heads'), may hold values from -3 to 3
- gate_gain: float32 [2, 512], P(None, 'heads'), may hold values from 0.5 to 1.5
- out_w: bfloat16 [2, 512, 2560], P(None, 'heads'), may hold values from -0.375 to 0.375
- ssm_state: float32 [2, 192, 8, 64, 128], P(None, 'batch', 'heads'), may hold values from -1.6 to 1.6
- conv_x_state: bfloat16 [2, 192, 3, 512], P(None, 'batch', None, 'heads'), may hold values from -6 to 6
- conv_bc_state: bfloat16 [2, 192, 3, 256], P(None, 'batch', None, 'heads'), may hold values from -6 to 6
Outputs:
- hidden_out: bfloat16 [1536, 2560], P('batch', 'heads')
- new_ssm: float32 [2, 192, 8, 64, 128], P(None, 'batch', 'heads')
- new_conv_x: bfloat16 [2, 192, 3, 512], P(None, 'batch', None, 'heads')
- new_conv_bc: bfloat16 [2, 192, 3, 256], P(None, 'batch', None, 'heads')
Inputs may be any that keep to these rules, and one draw needn't show every extreme that they name: `accepted`: the number of a sequence's draft tokens that are kept, counted from the first.
All inputs are finite; a program needn't handle non-finite values.
Results may differ from a plain program's by a relative error of at most 0.015.
Values may be sent and summed in bfloat16 or wider, within the bound.
A program may use at most 128 MiB of HBM per device.

v0:
```python
import jax
import jax.numpy as jnp
from jax import lax
from jax.sharding import PartitionSpec as P

LAYERS = 2


EPS = 1e-05


def rms_scale(total, count):
    return lax.rsqrt(total / count + EPS)


def convolve(window, weight, bias, count):
    weight = weight.astype(jnp.float32)
    acc = window[:, 0:count] * weight[0]
    for k in range(1, weight.shape[0]):
        acc = acc + window[:, k : k + count] * weight[k]
    return jax.nn.silu(acc + bias.astype(jnp.float32))


def keep_rows(window, accepted, kept_rows):
    last_start = window.shape[1] - kept_rows
    kept = window[:, 1 : 1 + kept_rows]
    for start in range(2, last_start + 1):
        kept = jnp.where(
            (accepted == start)[:, None, None], window[:, start : start + kept_rows], kept
        )
    return kept


def recur(decay, step, values, bmat, cmat, skip, state, accepted):
    kept = state
    outputs = []
    for t in range(values.shape[1]):
        state = (
            decay[:, t, None, None] * state
            + (step[:, t, None] * values[:, t])[:, :, None] * bmat[:, t, None, :]
        )
        outputs.append(jnp.sum(state * cmat[:, t, None, :], axis=-1) + skip * values[:, t])
        kept = jnp.where((accepted == t + 1)[:, None, None], state, kept)
    return (jnp.stack(outputs, 1), kept)


def spread_terms(u_rows, scale, weight):
    product = lax.dot_general(
        weight, u_rows, (((0,), (1,)), ((), ())), preferred_element_type=jnp.float32
    )
    return product * scale[None, :]


def token_scale(local_sq, inner):
    return rms_scale(lax.psum(local_sq, "heads"), inner)


def local(
    draft_ids,
    accepted,
    embedding,
    norm_gain,
    w_zx,
    w_dt,
    w_bc,
    dt_bias,
    decay_rate,
    skip_weight,
    conv_x_w,
    conv_x_b,
    conv_bc_w,
    conv_bc_b,
    gate_gain,
    out_w,
    ssm_state,
    conv_x_state,
    conv_bc_state,
):
    seq_rows, draft = draft_ids.shape
    heads_here = w_zx.shape[2]
    width = w_zx.shape[3] // 2
    local_inner = heads_here * width
    own_cols = embedding.shape[1]
    model = own_cols * lax.axis_size("heads")
    inner = local_inner * lax.axis_size("heads")
    bc_here = w_bc.shape[2]
    kernel = conv_x_w.shape[1]
    recur_heads = jax.vmap(recur, in_axes=(2, 2, 2, None, None, 0, 1, None), out_axes=(2, 1))
    whole_bc = (
        lax.all_gather(w_bc, "heads", axis=2, tiled=True),
        lax.all_gather(conv_bc_w, "heads", axis=2, tiled=True),
        lax.all_gather(conv_bc_b, "heads", axis=1, tiled=True),
        lax.all_gather(conv_bc_state, "heads", axis=3, tiled=True),
    )
    saved_state, saved_x, saved_bc = ([], [], [])

    def mixer(layer, stream):
        value = stream.astype(jnp.float32)
        normed = (
            value * rms_scale(jnp.sum(value * value, -1, keepdims=True), model) * norm_gain[layer]
        ).astype(jnp.bfloat16)
        zx = jnp.dot(
            normed, w_zx[layer].reshape(model, -1), preferred_element_type=jnp.float32
        ).astype(jnp.bfloat16)
        zx = zx.reshape(seq_rows, draft, heads_here, 2, width)
        gate_z = zx[:, :, :, 0].astype(jnp.float32)
        values = zx[:, :, :, 1].reshape(seq_rows, draft, local_inner)
        dt_raw = (
            jnp.dot(normed, w_dt[layer], preferred_element_type=jnp.float32)
            .astype(jnp.bfloat16)
            .reshape(seq_rows, draft, heads_here)
        )
        bc = (
            jnp.dot(normed, whole_bc[0][layer], preferred_element_type=jnp.float32)
            .astype(jnp.bfloat16)
            .reshape(seq_rows, draft, -1)
        )
        window_bc = jnp.concatenate([whole_bc[3][layer], bc], axis=1)
        bcc = convolve(
            window_bc.astype(jnp.float32), whole_bc[1][layer], whole_bc[2][layer], draft
        ).astype(jnp.bfloat16)
        kept_bc = keep_rows(window_bc, accepted, kernel - 1)
        bcc = lax.optimization_barrier(bcc).astype(jnp.float32)
        kept_bc = lax.dynamic_slice_in_dim(kept_bc, lax.axis_index("heads") * bc_here, bc_here, 2)
        states = bcc.shape[2] // 2
        bmat = bcc[..., :states]
        cmat = bcc[..., states:]
        window_x = jnp.concatenate([conv_x_state[layer], values], axis=1)
        xc = convolve(
            window_x.astype(jnp.float32), conv_x_w[layer], conv_x_b[layer], draft
        ).reshape(seq_rows, draft, heads_here, width)
        step = jax.nn.softplus(dt_raw.astype(jnp.float32) + dt_bias[layer])
        decay = jnp.exp(-step * decay_rate[layer])
        outputs, kept = recur_heads(
            decay, step, xc, bmat, cmat, skip_weight[layer], ssm_state[layer], accepted
        )
        saved_state.append(kept)
        saved_x.append(keep_rows(window_x, accepted, kernel - 1))
        saved_bc.append(kept_bc)
        gated = outputs * jax.nn.silu(gate_z)
        local_sq = jnp.sum(gated * gated, axis=(2, 3)).reshape(-1)
        u_rows = (
            (gated.reshape(seq_rows, draft, local_inner) * gate_gain[layer])
            .astype(jnp.bfloat16)
            .reshape(-1, local_inner)
        )
        return (u_rows, local_sq)

    part = embedding[draft_ids.reshape(-1)]
    stream = lax.all_gather(part, "heads", axis=1, tiled=True)
    where_cols = lax.axis_index("heads") * own_cols
    result = part
    for layer in range(LAYERS):
        u_rows, local_sq = mixer(layer, stream)
        scale = token_scale(local_sq, inner)
        if layer + 1 < LAYERS:
            term = (
                jnp.dot(u_rows, out_w[layer], preferred_element_type=jnp.float32) * scale[:, None]
            )
            total = lax.psum(term, "heads")
            stream = (stream.astype(jnp.float32) + total).astype(jnp.bfloat16)
        else:
            mine = lax.psum_scatter(
                spread_terms(u_rows, scale, out_w[layer]), "heads", scatter_dimension=0, tiled=True
            )
            own_stream = lax.dynamic_slice_in_dim(stream, where_cols, own_cols, 1)
            result = (own_stream.astype(jnp.float32) + mine.T).astype(jnp.bfloat16)
    return (result, jnp.stack(saved_state), jnp.stack(saved_x), jnp.stack(saved_bc))


def solution(mesh):
    placed = (
        P("batch", None),
        P("batch"),
        P(None, "heads"),
        P(),
        P(None, None, "heads", None),
        P(None, None, "heads"),
        P(None, None, "heads"),
        P(None, "heads"),
        P(None, "heads"),
        P(None, "heads"),
        P(None, None, "heads"),
        P(None, "heads"),
        P(None, None, "heads"),
        P(None, "heads"),
        P(None, "heads"),
        P(None, "heads", None),
        P(None, "batch", "heads", None, None),
        P(None, "batch", None, "heads"),
        P(None, "batch", None, "heads"),
    )
    return jax.shard_map(
        local,
        mesh=mesh,
        in_specs=placed,
        out_specs=(
            P("batch", "heads"),
            P(None, "batch", "heads", None, None),
            P(None, "batch", None, "heads"),
            P(None, "batch", None, "heads"),
        ),
        check_vma=False,
    )
```

profile of v0, /device:TPU:0, one launch (start us, length us, event | category | flops | bytes accessed | tf_op | source)
XLA Modules:
  0.0 371.8 jit_solution(4346947506731001234)
XLA Ops:
  7.2 43.7 %copy.113 = bf16[50280,320]{1,0:T(8,128)(2,1)} copy(bf16[50280,320]{0,1:T(8,128)(2,1)} %param.21) | data formatting | bytes 64358400 | tf_op args[2]
  51.2 7.8 %gather_fusion = bf16[384,320]{1,0:T(8,128)(2,1)S(1)} fusion(bf16[50280,320]{1,0:T(8,128)(2,1)} %copy.113, s32[1024]{0:T(1024)S(1)} %pad_clamp_fusion), kind=kCustom, calls=%fused_computation | custom fusion | bytes 493056 | tf_op jit(solution)/shard_map/gather | solution.py:149
  59.0 0.9 copy.114
  60.0 0.7 all-gather.5.cloned.1.call-update
  60.8 16.7 %all_gather.16 = bf16[2,48,3,256]{1,3,2,0:T(8,128)(2,1)S(1)} all-gather(bf16[2,48,3,32]{1,3,2,0:T(8,128)(2,1)S(1)} %copy-done.48), channel_id=1, replica_groups=mesh['batch'=4,'heads'=8] {'heads'}, dimensions={3}, use_global_device_ids=true | all-gather | bytes 165888 | tf_op jit(solution)/shard_map/all_gather | solution.py:93
  77.8 15.2 %all_gather.18 = bf16[2,4,256]{1,0,2:T(2,128)(2,1)S(1)} all-gather(bf16[2,4,32]{1,0,2:T(2,128)(2,1)S(1)} %copy.118), channel_id=1, replica_groups=mesh['batch'=4,'heads'=8] {'heads'}, dimensions={2}, use_global_device_ids=true | all-gather | bytes 4608 | tf_op jit(solution)/shard_map/all_gather | solution.py:91
  93.0 12.0 %all-gather.1 = bf16[8,32,2]{1,2,0:T(2,128)(2,1)S(1)} all-gather(bf16[1,32,2]{1,2,0:T(2,128)(2,1)S(1)} %bitcast.580), channel_id=1, replica_groups=mesh['batch'=4,'heads'=8] {'heads'}, dimensions={0}, use_global_device_ids=true | all-gather | bytes 1152 | tf_op jit(solution)/shard_map/all_gather | solution.py:92
  107.1 2.9 slice_reduce_fusion.7
  111.2 2.7 copy.115
  114.5 0.8 copy-done.83
  115.3 0.7 convolution_convert_fusion.1
  116.5 0.7 convolution_reduce_fusion.1
  118.0 0.7 multiply_exponential_fusion.1
  119.6 7.5 %all-gather.5.cloned.1.call-done = bf16[2,2560,256]{1,2,0:T(8,128)(2,1)} async-done(((bf16[2,2560,32]{1,2,0:T(8,128)(2,1)}), bf16[2,2560,256]{1,2,0:T(8,128)(2,1)}) %all-gather.5.cloned.1.call-update) | async-done | bytes 2621456 | tf_op jit(solution)/shard_map/all_gather | solution.py:90
  127.2 2.0 fusion.15
  130.1 1.1 copy-done
  131.2 4.1 %multiply_add_fusion.8 = (f32[1,48,64,128]{3,2,1,0:T(8,128)S(1)}, f32[1,48,64,128]{3,2,1,0:T(8,128)S(1)}, f32[48,64]{1,0:T(8,128)S(1)}, f32[48,64]{1,0:T(8,128)S(1)}) fusion(f32[48,128]{1,0:T(8,128)S(1)} %bitcast.537, f32[48,64]{1,0:T(8,128)S(1)} %get-tuple-element.186, f32[48]{0:T(128)S(1)} %get-tuple-element.237, f32[48,128]{1,0:T(8,128)S(1)} %bitcast.525, ...), kind=kLoop, calls=%fused_computation.43 | loop fusion | flops 7464960 | bytes 4977600 | tf_op jit(solution)/shard_map/vmap()/add | solution.py:39
  136.0 1.6 multiply_reduce_fusion.12
  139.4 3.7 multiply_reduce_fusion.8
  145.8 15.0 %psum.21 = f32[384]{0:T(512)S(1)} all-reduce(f32[384]{0:T(512)S(1)} %reshape.2511), channel_id=1, replica_groups=mesh['batch'=4,'heads'=8] {'heads'}, use_global_device_ids=true, to_apply=%region_10.11 | all-reduce | flops 384 | bytes 3072 | tf_op jit(solution)/shard_map/psum | solution.py:55
  160.9 3.5 convolution_multiply_fusion.1
  164.8 0.8 copy.125
  165.5 2.9 slice_reduce_fusion.3
  168.5 85.9 %all-reduce.2.cloned.1.call-done = f32[384,2560]{1,0:T(8,128)} async-done(((f32[384,2560]{1,0:T(8,128)}), f32[384,2560]{1,0:T(8,128)}) %all-reduce.2.cloned.1.call-update) | async-done | bytes 3932176 | tf_op jit(solution)/shard_map/psum | solution.py:160
  254.3 2.9 fusion.1
  257.3 0.7 convolution_convert_fusion
  258.5 0.7 convolution_reduce_fusion
  259.4 1.0 fusion.121
  261.1 0.8 fusion.128
  261.9 0.8 fusion.129
  264.7 2.1 fusion.14
  267.6 1.0 bitcast_multiply_fusion.2
  268.8 4.1 %multiply_add_fusion.2 = (f32[1,48,64,128]{3,2,1,0:T(8,128)S(1)}, f32[1,48,64,128]{3,2,1,0:T(8,128)S(1)}, f32[48,64]{1,0:T(8,128)S(1)}, f32[48,64]{1,0:T(8,128)S(1)}) fusion(f32[48,128]{1,0:T(8,128)S(1)} %bitcast.551, f32[48,64]{1,0:T(8,128)S(1)} %get-tuple-element.160, f32[48]{0:T(128)S(1)} %get-tuple-element.51, f32[48,128]{1,0:T(8,128)S(1)} %bitcast.528, ...), kind=kLoop, calls=%fused_computation.29 | loop fusion | flops 7464960 | bytes 4977600 | tf_op jit(solution)/shard_map/vmap()/add | solution.py:39
  273.0 1.2 constant_dynamic-update-slice_fusion.23
  274.2 1.6 multiply_reduce_fusion.4
  275.9 1.2 constant_dynamic-update-slice_fusion.22
  277.1 1.2 constant_dynamic-update-slice_fusion.21
  278.3 1.2 constant_dynamic-update-slice_fusion.20
  279.5 3.7 multiply_reduce_fusion
  283.2 1.2 constant_dynamic-update-slice_fusion.19
  284.4 1.2 constant_dynamic-update-slice_fusion.18
  285.6 1.2 constant_dynamic-update-slice_fusion.17
  286.7 1.9 constant_dynamic-update-slice_fusion.16
  288.8 0.7 copy.135
  289.5 0.8 reshape.2516
  290.3 15.6 %psum.23 = f32[384]{0:T(512)S(1)} all-reduce(f32[384]{0:T(512)S(1)} %reshape.2516), channel_id=1, replica_groups=mesh['batch'=4,'heads'=8] {'heads'}, use_global_device_ids=true, to_apply=%region_22.23 | all-reduce | flops 384 | bytes 3072 | tf_op jit(solution)/shard_map/psum | solution.py:55
  306.0 1.1 fusion.71
  307.1 3.5 fusion
  310.6 5.6 %copy.139 = f32[2560,384]{1,0:T(8,128)} copy(f32[2560,384]{0,1:T(8,128)} %fusion) | data formatting | bytes 7864320
  316.2 1.2 broadcast_compare_fusion.7
  317.5 1.7 fusion.105
  319.1 1.4 fusion.119
  320.6 0.7 dynamic-slice_select_fusion.6
  321.3 0.7 copy.136
  322.0 9.0 %select_select_fusion.1 = f32[1,48,1,64,128]{4,3,2,1,0:T(8,128)} fusion(f32[2,48,1,64,128]{4,3,2,1,0:T(8,128)S(1)} %copy-done.1, f32[48,128]{1,0:T(8,128)} %bitcast.536, f32[48,64]{1,0:T(8,128)} %copy-done.34, f32[48,128]{1,0:T(8,128)} %bitcast.534, f32[48,64]{1,0:T(8,128)} %copy-done.35, f32[48,128]{1,0:T(8,128)} %bitcast.532, f32[48,64]{1,0:T(8,128)} %copy-done.33, ...), kind=kLoop, calls=%fused_computation.22 | loop fusion | flops 12582912 | bytes 3442560 | tf_op jit(solution)/shard_map/vmap(jit(_where))/select_n | solution.py:43
  332.4 1.4 pad_maximum_fusion.6
  333.8 0.9 fusion.106
  334.7 1.4 pad_maximum_fusion.5
  336.1 8.2 %select_select_fusion = f32[1,48,1,64,128]{4,3,2,1,0:T(8,128)S(1)} fusion(f32[2,48,1,64,128]{4,3,2,1,0:T(8,128)S(1)} %copy-done.1, f32[48,128]{1,0:T(8,128)} %bitcast.550, f32[48,64]{1,0:T(8,128)} %copy-done.40, f32[48,128]{1,0:T(8,128)} %bitcast.548, f32[48,64]{1,0:T(8,128)} %copy-done.42, f32[48,128]{1,0:T(8,128)} %bitcast.546, f32[48,64]{1,0:T(8,128)} %copy-done.41, ...), kind=kLoop, calls=%fused_computation.21 | loop fusion | flops 12582912 | bytes 3442560 | tf_op jit(solution)/shard_map/vmap(jit(_where))/select_n | solution.py:43
  344.4 1.9 pad_maximum_fusion
  346.3 15.7 %reduce-scatter.4.cloned.1.call-done = f32[320,384]{1,0:T(8,128)} async-done(((f32[2560,384]{1,0:T(8,128)}), f32[320,384]{1,0:T(8,128)}) %reduce-scatter.4.cloned.1.call-update) | async-done | bytes 491536
  362.0 1.3 copy.140
  363.2 1.2 fusion.20
  364.4 0.9 copy.138
  (243 shorter events, 18.1 us)
Async XLA Ops:
  7.2 43.8 %copy-start.73 = (s32[48,8]{0,1:T(8,128)S(1)}, s32[48,8]{0,1:T(8,128)}, u32[]{:S(2)}) copy-start(s32[48,8]{0,1:T(8,128)} %param.19) | copy-start | bytes 4612
  7.2 104.1 %all-gather.7.cloned.1.call-start = ((), (), s32[]{:S(2)}) async-start(), calls=%async_computation.3 | async-start | bytes 2211840 | tf_op jit(solution)/shard_map/all_gather | solution.py:150
  51.2 9.6 %copy-start.48 = (bf16[2,48,3,32]{1,3,2,0:T(8,128)(2,1)S(1)}, bf16[2,48,3,32]{1,3,2,0:T(8,128)(2,1)}, u32[]{:S(2)}) copy-start(bf16[2,48,3,32]{1,3,2,0:T(8,128)(2,1)} %param.37) | copy-start | bytes 55300
  58.9 18.7 %copy-start.75 = (bf16[2,4,32]{2,1,0:T(4,128)(2,1)S(1)}, bf16[2,4,32]{2,1,0:T(4,128)(2,1)}, u32[]{:S(2)}) copy-start(bf16[2,4,32]{2,1,0:T(4,128)(2,1)} %param.31) | copy-start | bytes 1540
  59.0 34.0 %copy-start.82 = (bf16[2,32]{1,0:T(2,128)(2,1)S(1)}, bf16[2,32]{1,0:T(2,128)(2,1)}, u32[]{:S(2)}) copy-start(bf16[2,32]{1,0:T(2,128)(2,1)} %param.32) | copy-start | bytes 388
  59.0 46.1 %copy-start.77 = (f32[2,1]{0,1:T(1,128)S(1)}, f32[2,1]{0,1:T(1,128)}, u32[]{:S(2)}) copy-start(f32[2,1]{0,1:T(1,128)} %param.26) | copy-start | bytes 28
  59.0 46.7 %copy-start.78 = (f32[2,1]{0,1:T(1,128)S(1)}, f32[2,1]{0,1:T(1,128)}, u32[]{:S(2)}) copy-start(f32[2,1]{0,1:T(1,128)} %param.27) | copy-start | bytes 28
  59.0 47.3 %copy-start.79 = (f32[2,1]{0,1:T(1,128)S(1)}, f32[2,1]{0,1:T(1,128)}, u32[]{:S(2)}) copy-start(f32[2,1]{0,1:T(1,128)} %param.28) | copy-start | bytes 28
  59.0 47.8 %copy-start.55 = (f32[2,2560]{1,0:T(2,128)S(1)}, f32[2,2560]{1,0:T(2,128)}, u32[]{:S(2)}) copy-start(f32[2,2560]{1,0:T(2,128)} %param.22) | copy-start | bytes 61444
  59.9 50.1 %copy-start.80 = (bf16[2,64]{1,0:T(2,128)(2,1)S(1)}, bf16[2,64]{1,0:T(2,128)(2,1)}, u32[]{:S(2)}) copy-start(bf16[2,64]{1,0:T(2,128)(2,1)} %param.30) | copy-start | bytes 772
  59.9 50.1 %copy-start.81 = (f32[2,64]{1,0:T(2,128)S(1)}, f32[2,64]{1,0:T(2,128)}, u32[]{:S(2)}) copy-start(f32[2,64]{1,0:T(2,128)} %param.33) | copy-start | bytes 1540
  59.9 51.2 %copy-start.76 = (bf16[2,4,64]{2,1,0:T(4,128)(2,1)S(1)}, bf16[2,4,64]{2,1,0:T(4,128)(2,1)}, u32[]{:S(2)}) copy-start(bf16[2,4,64]{2,1,0:T(4,128)(2,1)} %param.29) | copy-start | bytes 3076
  59.9 51.2 %copy-start.47 = (bf16[2,48,3,64]{3,1,2,0:T(8,128)(2,1)S(1)}, bf16[2,48,3,64]{3,1,2,0:T(8,128)(2,1)}, u32[]{:S(2)}) copy-start(bf16[2,48,3,64]{3,1,2,0:T(8,128)(2,1)} %param.36) | copy-start | bytes 110596
  59.9 67.2 %all-gather.5.cloned.1.call-start = ((), (), s32[]{:S(2)}) async-start(), calls=%async_computation.1 | async-start | bytes 2949120 | tf_op jit(solution)/shard_map/all_gather | solution.py:90
  60.7 193.6 %all-reduce.2.cloned.1.call-start = ((), (), s32[]{:S(2)}) async-start(), calls=%async_computation.2 | async-start | bytes 7864320 | tf_op jit(solution)/shard_map/psum | solution.py:160
  77.7 51.5 %copy-start.10 = (bf16[48,3,256]{2,1,0:T(4,128)(2,1)}, bf16[48,3,256]{2,1,0:T(4,128)(2,1)S(1)}, u32[]{:S(2)}) copy-start(bf16[48,3,256]{2,1,0:T(4,128)(2,1)S(1)} %copy.117) | copy-start | bytes 221188
  111.2 8.1 %copy-start.18 = (bf16[48,3,64]{2,0,1:T(8,128)(2,1)}, bf16[48,3,64]{2,0,1:T(8,128)(2,1)S(1)}, u32[]{:S(2)}) copy-start(bf16[48,3,64]{2,0,1:T(8,128)(2,1)S(1)} %get-tuple-element.194) | copy-start | bytes 55300
  111.2 149.2 %copy-start.17 = (bf16[48,3,64]{2,0,1:T(8,128)(2,1)}, bf16[48,3,64]{2,0,1:T(8,128)(2,1)S(1)}, u32[]{:S(2)}) copy-start(bf16[48,3,64]{2,0,1:T(8,128)(2,1)S(1)} %get-tuple-element.193) | copy-start | bytes 55300
  119.2 10.8 %copy-start.58 = (f32[48]{0:T(128)}, f32[48]{0:T(128)S(1)}, u32[]{:S(2)}) copy-start(f32[48]{0:T(128)S(1)} %get-tuple-element.233) | copy-start | bytes 580
  119.2 10.8 %copy-start.59 = (f32[48]{0:T(128)}, f32[48]{0:T(128)S(1)}, u32[]{:S(2)}) copy-start(f32[48]{0:T(128)S(1)} %get-tuple-element.234) | copy-start | bytes 580
  119.2 10.8 %copy-start.60 = (f32[48]{0:T(128)}, f32[48]{0:T(128)S(1)}, u32[]{:S(2)}) copy-start(f32[48]{0:T(128)S(1)} %get-tuple-element.235) | copy-start | bytes 580
  119.2 10.8 %copy-start.61 = (f32[48]{0:T(128)}, f32[48]{0:T(128)S(1)}, u32[]{:S(2)}) copy-start(f32[48]{0:T(128)S(1)} %get-tuple-element.237) | copy-start | bytes 580
  119.2 16.7 %copy-start.56 = (f32[48]{0:T(128)}, f32[48]{0:T(128)S(1)}, u32[]{:S(2)}) copy-start(f32[48]{0:T(128)S(1)} %get-tuple-element.236) | copy-start | bytes 580
  119.2 20.1 %copy-start.66 = (f32[48]{0:T(128)}, f32[48]{0:T(128)S(1)}, u32[]{:S(2)}) copy-start(f32[48]{0:T(128)S(1)} %get-tuple-element.238) | copy-start | bytes 580
  119.2 20.1 %copy-start.67 = (f32[48]{0:T(128)}, f32[48]{0:T(128)S(1)}, u32[]{:S(2)}) copy-start(f32[48]{0:T(128)S(1)} %get-tuple-element.239) | copy-start | bytes 580
  119.2 20.1 %copy-start.68 = (f32[48]{0:T(128)}, f32[48]{0:T(128)S(1)}, u32[]{:S(2)}) copy-start(f32[48]{0:T(128)S(1)} %get-tuple-element.240) | copy-start | bytes 580
  119.6 10.5 %copy-start.36 = (f32[48,64]{1,0:T(8,128)}, f32[48,64]{1,0:T(8,128)S(1)}, u32[]{:S(2)}) copy-start(f32[48,64]{1,0:T(8,128)S(1)} %get-tuple-element.186) | copy-start | bytes 36868
  119.6 10.5 %copy-start.37 = (f32[48,64]{1,0:T(8,128)}, f32[48,64]{1,0:T(8,128)S(1)}, u32[]{:S(2)}) copy-start(f32[48,64]{1,0:T(8,128)S(1)} %get-tuple-element.188) | copy-start | bytes 36868
  119.6 10.5 %copy-start.38 = (f32[48,64]{1,0:T(8,128)}, f32[48,64]{1,0:T(8,128)S(1)}, u32[]{:S(2)}) copy-start(f32[48,64]{1,0:T(8,128)S(1)} %get-tuple-element.189) | copy-start | bytes 36868
  119.6 10.5 %copy-start.39 = (f32[48,64]{1,0:T(8,128)}, f32[48,64]{1,0:T(8,128)S(1)}, u32[]{:S(2)}) copy-start(f32[48,64]{1,0:T(8,128)S(1)} %get-tuple-element.190) | copy-start | bytes 36868
  119.6 16.3 %copy-start.15 = (f32[48,64]{1,0:T(8,128)}, f32[48,64]{1,0:T(8,128)S(1)}, u32[]{:S(2)}) copy-start(f32[48,64]{1,0:T(8,128)S(1)} %get-tuple-element.187) | copy-start | bytes 36868
  119.6 19.8 %copy-start.33 = (f32[48,64]{1,0:T(8,128)}, f32[48,64]{1,0:T(8,128)S(1)}, u32[]{:S(2)}) copy-start(f32[48,64]{1,0:T(8,128)S(1)} %get-tuple-element.183) | copy-start | bytes 36868
  119.6 19.8 %copy-start.34 = (f32[48,64]{1,0:T(8,128)}, f32[48,64]{1,0:T(8,128)S(1)}, u32[]{:S(2)}) copy-start(f32[48,64]{1,0:T(8,128)S(1)} %get-tuple-element.184) | copy-start | bytes 36868
  119.6 19.8 %copy-start.35 = (f32[48,64]{1,0:T(8,128)}, f32[48,64]{1,0:T(8,128)S(1)}, u32[]{:S(2)}) copy-start(f32[48,64]{1,0:T(8,128)S(1)} %get-tuple-element.185) | copy-start | bytes 36868
  129.9 5.4 %copy-start.22 = (f32[48,1,128]{2,1,0:T(1,128)}, f32[48,1,128]{2,1,0:T(1,128)S(1)}, u32[]{:S(2)}) copy-start(f32[48,1,128]{2,1,0:T(1,128)S(1)} %get-tuple-element.174) | copy-start | bytes 73732
  129.9 5.4 %copy-start.23 = (f32[48,1,128]{2,1,0:T(1,128)}, f32[48,1,128]{2,1,0:T(1,128)S(1)}, u32[]{:S(2)}) copy-start(f32[48,1,128]{2,1,0:T(1,128)S(1)} %get-tuple-element.178) | copy-start | bytes 73732
  129.9 5.4 %copy-start.24 = (f32[48,1,128]{2,1,0:T(1,128)}, f32[48,1,128]{2,1,0:T(1,128)S(1)}, u32[]{:S(2)}) copy-start(f32[48,1,128]{2,1,0:T(1,128)S(1)} %get-tuple-element.180) | copy-start | bytes 73732
  129.9 5.4 %copy-start.25 = (f32[48,1,128]{2,1,0:T(1,128)}, f32[48,1,128]{2,1,0:T(1,128)S(1)}, u32[]{:S(2)}) copy-start(f32[48,1,128]{2,1,0:T(1,128)S(1)} %get-tuple-element.181) | copy-start | bytes 73732
  129.9 6.0 %copy-start.13 = (f32[48,1,128]{2,1,0:T(1,128)}, f32[48,1,128]{2,1,0:T(1,128)S(1)}, u32[]{:S(2)}) copy-start(f32[48,1,128]{2,1,0:T(1,128)S(1)} %get-tuple-element.176) | copy-start | bytes 73732
  130.0 9.5 %copy-start.19 = (f32[48,1,128]{2,1,0:T(1,128)}, f32[48,1,128]{2,1,0:T(1,128)S(1)}, u32[]{:S(2)}) copy-start(f32[48,1,128]{2,1,0:T(1,128)S(1)} %get-tuple-element.170) | copy-start | bytes 73732
  130.0 9.5 %copy-start.20 = (f32[48,1,128]{2,1,0:T(1,128)}, f32[48,1,128]{2,1,0:T(1,128)S(1)}, u32[]{:S(2)}) copy-start(f32[48,1,128]{2,1,0:T(1,128)S(1)} %get-tuple-element.171) | copy-start | bytes 73732
  130.0 9.5 %copy-start.21 = (f32[48,1,128]{2,1,0:T(1,128)}, f32[48,1,128]{2,1,0:T(1,128)S(1)}, u32[]{:S(2)}) copy-start(f32[48,1,128]{2,1,0:T(1,128)S(1)} %get-tuple-element.172) | copy-start | bytes 73732
  164.5 197.5 %reduce-scatter.4.cloned.1.call-start = ((), (), s32[]{:S(2)}) async-start(), calls=%async_computation.4 | async-start | bytes 4423680
  264.6 9.6 %copy-start.57 = (f32[48]{0:T(128)}, f32[48]{0:T(128)S(1)}, u32[]{:S(2)}) copy-start(f32[48]{0:T(128)S(1)} %get-tuple-element.52) | copy-start | bytes 580
  264.6 14.8 %copy-start.69 = (f32[48]{0:T(128)}, f32[48]{0:T(128)S(1)}, u32[]{:S(2)}) copy-start(f32[48]{0:T(128)S(1)} %get-tuple-element.48) | copy-start | bytes 580
  264.6 14.8 %copy-start.70 = (f32[48]{0:T(128)}, f32[48]{0:T(128)S(1)}, u32[]{:S(2)}) copy-start(f32[48]{0:T(128)S(1)} %get-tuple-element.49) | copy-start | bytes 580
  264.6 14.8 %copy-start.71 = (f32[48]{0:T(128)}, f32[48]{0:T(128)S(1)}, u32[]{:S(2)}) copy-start(f32[48]{0:T(128)S(1)} %get-tuple-element.50) | copy-start | bytes 580
  267.5 5.5 %copy-start.29 = (f32[48,1,128]{2,1,0:T(1,128)}, f32[48,1,128]{2,1,0:T(1,128)S(1)}, u32[]{:S(2)}) copy-start(f32[48,1,128]{2,1,0:T(1,128)S(1)} %get-tuple-element.149) | copy-start | bytes 73732
  267.5 5.5 %copy-start.30 = (f32[48,1,128]{2,1,0:T(1,128)}, f32[48,1,128]{2,1,0:T(1,128)S(1)}, u32[]{:S(2)}) copy-start(f32[48,1,128]{2,1,0:T(1,128)S(1)} %get-tuple-element.153) | copy-start | bytes 73732
  267.5 5.5 %copy-start.31 = (f32[48,1,128]{2,1,0:T(1,128)}, f32[48,1,128]{2,1,0:T(1,128)S(1)}, u32[]{:S(2)}) copy-start(f32[48,1,128]{2,1,0:T(1,128)S(1)} %get-tuple-element.155) | copy-start | bytes 73732
  267.5 5.5 %copy-start.32 = (f32[48,1,128]{2,1,0:T(1,128)}, f32[48,1,128]{2,1,0:T(1,128)S(1)}, u32[]{:S(2)}) copy-start(f32[48,1,128]{2,1,0:T(1,128)S(1)} %get-tuple-element.156) | copy-start | bytes 73732
  267.5 6.7 %copy-start.14 = (f32[48,1,128]{2,1,0:T(1,128)}, f32[48,1,128]{2,1,0:T(1,128)S(1)}, u32[]{:S(2)}) copy-start(f32[48,1,128]{2,1,0:T(1,128)S(1)} %get-tuple-element.151) | copy-start | bytes 73732
  267.5 11.9 %copy-start.26 = (f32[48,1,128]{2,1,0:T(1,128)}, f32[48,1,128]{2,1,0:T(1,128)S(1)}, u32[]{:S(2)}) copy-start(f32[48,1,128]{2,1,0:T(1,128)S(1)} %get-tuple-element.145) | copy-start | bytes 73732
  267.5 11.9 %copy-start.27 = (f32[48,1,128]{2,1,0:T(1,128)}, f32[48,1,128]{2,1,0:T(1,128)S(1)}, u32[]{:S(2)}) copy-start(f32[48,1,128]{2,1,0:T(1,128)S(1)} %get-tuple-element.146) | copy-start | bytes 73732
  267.5 11.9 %copy-start.28 = (f32[48,1,128]{2,1,0:T(1,128)}, f32[48,1,128]{2,1,0:T(1,128)S(1)}, u32[]{:S(2)}) copy-start(f32[48,1,128]{2,1,0:T(1,128)S(1)} %get-tuple-element.147) | copy-start | bytes 73732
  268.6 10.9 %copy-start.40 = (f32[48,64]{1,0:T(8,128)}, f32[48,64]{1,0:T(8,128)S(1)}, u32[]{:S(2)}) copy-start(f32[48,64]{1,0:T(8,128)S(1)} %bitcast_multiply_fusion.2) | copy-start | bytes 36868
  268.7 5.5 %copy-start.16 = (f32[48,64]{1,0:T(8,128)}, f32[48,64]{1,0:T(8,128)S(1)}, u32[]{:S(2)}) copy-start(f32[48,64]{1,0:T(8,128)S(1)} %get-tuple-element.161) | copy-start | bytes 36868
  268.7 10.7 %copy-start.41 = (f32[48,64]{1,0:T(8,128)}, f32[48,64]{1,0:T(8,128)S(1)}, u32[]{:S(2)}) copy-start(f32[48,64]{1,0:T(8,128)S(1)} %get-tuple-element.158) | copy-start | bytes 36868
  268.7 10.7 %copy-start.42 = (f32[48,64]{1,0:T(8,128)}, f32[48,64]{1,0:T(8,128)S(1)}, u32[]{:S(2)}) copy-start(f32[48,64]{1,0:T(8,128)S(1)} %get-tuple-element.159) | copy-start | bytes 36868
  275.9 12.8 %copy-start.8 = (bf16[48,8,1,1,64]{4,3,1,0,2:T(2,128)(2,1)S(1)}, bf16[48,8,1,1,64]{4,3,1,0,2:T(2,128)(2,1)}, u32[]{:S(2)}) copy-start(bf16[48,8,1,1,64]{4,3,1,0,2:T(2,128)(2,1)} %get-tuple-element.140) | copy-start | bytes 147460
  275.9 30.1 %copy-start.74 = (f32[64]{0:T(128)S(1)}, f32[64]{0:T(128)}, u32[]{:S(2)}) copy-start(f32[64]{0:T(128)} %get-tuple-element.209) | copy-start | bytes 772
  322.0 9.0 %copy-start.12 = (bf16[48,3,256]{2,1,0:T(4,128)(2,1)S(1)}, bf16[48,3,256]{2,1,0:T(4,128)(2,1)}, u32[]{:S(2)}) copy-start(bf16[48,3,256]{2,1,0:T(4,128)(2,1)} %copy.125) | copy-start | bytes 221188
  322.0 9.0 %copy-start.54 = (pred[48]{0:T(512)(128)(4,1)S(1)}, pred[48]{0:T(512)(128)(4,1)}, u32[]{:S(2)}) copy-start(pred[48]{0:T(512)(128)(4,1)} %copy-done.53) | copy-start | bytes 148
  336.1 8.3 %copy-start.2 = (f32[1,48,1,64,128]{4,3,2,1,0:T(8,128)S(1)}, f32[1,48,1,64,128]{4,3,2,1,0:T(8,128)}, u32[]{:S(2)}) copy-start(f32[1,48,1,64,128]{4,3,2,1,0:T(8,128)} %select_select_fusion.1) | copy-start | bytes 4718596
  (26 other events, 71.5 us)
Sparse Core Ops, SparseCore 0:
  60.0 32.7 all-gather.6
  94.4 32.7 all-gather.4
  164.6 89.6 all-reduce.1
  316.3 45.5 reduce-scatter.3
where the time goes:
time: 374 us; the launch traced here: 372 us
  waiting for transfers between devices  110 us (29%)
  local copies, waits for them, and re-layouts  81.7 us (22%)
  other arithmetic  75.7 us (20%)
  blocking collectives  74.6 us (20%)
  between operations  15.4 us (4%)
  matrix products  14.1 us (4%)
    psum x1, waiting for transfers between devices, local(): total = lax.psum(term, 'heads')  85.9 us
    unnamed x181, local copies, waits for them, and re-layouts  55.4 us
    psum x2, blocking collectives, token_scale(): return rms_scale(lax.psum(local_sq, 'heads'), inner)  30.7 us
    select_n x2, other arithmetic, recur(): kept = jnp.where((accepted == t + 1)[:, None, None], state, kept)  17.3 us
    all_gather x1, blocking collectives, local(): lax.all_gather(conv_bc_state, 'heads', axis=3, tiled=True)  16.7 us
    unnamed x5, waiting for transfers between devices  16.4 us
    all_gather x1, blocking collectives, local(): lax.all_gather(conv_bc_w, 'heads', axis=2, tiled=True)  15.2 us
    unnamed x14, other arithmetic  12.3 us
  transfers between devices with their start and end apart: 4, of which 3 were waited for; matrix products, arithmetic and copies ran while one was open for 13% of the time, Pallas kernels for 0%

commit v1 on v0

v1 whole, which is shorter than its diff:
```python
import functools

import jax
import jax.numpy as jnp
from jax import lax
from jax.experimental import pallas as pl
from jax.experimental.pallas import tpu as pltpu
from jax.sharding import PartitionSpec as P

LAYERS = 2
EPS = 1e-05
MESH = pl.DeviceIdType.MESH
CHUNK = 2048
VMEM_LIMIT = 60 * 1024 * 1024


def rms_scale(total, count):
    return lax.rsqrt(total / count + EPS)


def dot_tn(a, b):
    return lax.dot_general(a, b, (((0,), (0,)), ((), ())), preferred_element_type=jnp.float32)


def dot_nt(a, b):
    return lax.dot_general(a, b, (((1,), (1,)), ((), ())), preferred_element_type=jnp.float32)


def keep_rows(window, accepted, kept_rows):
    last_start = window.shape[1] - kept_rows
    kept = window[:, 1 : 1 + kept_rows]
    for start in range(2, last_start + 1):
        kept = jnp.where(
            (accepted == start)[:, None, None], window[:, start : start + kept_rows], kept
        )
    return kept


def greet(n):
    me = lax.axis_index("heads")
    barrier = pltpu.get_barrier_semaphore()
    for d in range(1, n):
        pl.semaphore_signal(
            barrier, inc=1, device_id={"heads": lax.rem(me + d, n)}, device_id_type=MESH
        )
    pl.semaphore_wait(barrier, n - 1)


class Gather:
    def __init__(self, n, src, out, send, recv, fsend, frecv):
        self.n, self.src, self.out = n, src, out
        self.send, self.recv, self.fsend, self.frecv = send, recv, fsend, frecv
        self.me = lax.axis_index("heads")
        self.core = lax.rem(self.me, 2)
        self.chip = self.me // 2
        self.chips = n // 2
        self.mate = self.me + 1 - 2 * self.core

    def slot(self, c, core):
        return 2 * lax.rem(self.chip + self.chips - c, self.chips) + core

    def copy(self, src, slot, device, send, recv):
        return pltpu.make_async_remote_copy(
            src_ref=src,
            dst_ref=self.out.at[slot],
            send_sem=send,
            recv_sem=recv,
            device_id={"heads": device},
            device_id_type=MESH,
        )

    def first(self, c):
        if c == 0:
            return self.copy(self.src, self.me, self.mate, self.send.at[0], self.recv.at[0])
        dst = 2 * lax.rem(self.chip + c, self.chips) + self.core
        return self.copy(self.src, self.me, dst, self.send.at[c], self.recv.at[c])

    def arrival(self, c):
        if c == 0:
            return self.copy(self.src, self.mate, self.mate, self.send.at[0], self.recv.at[0])
        slot = self.slot(c, self.core)
        return self.copy(self.src, slot, slot, self.send.at[c], self.recv.at[c])

    def forward(self, c):
        slot = self.slot(c, self.core)
        return self.copy(
            self.out.at[slot], slot, self.mate, self.fsend.at[c], self.frecv.at[c]
        )

    def forwarded(self, c):
        slot = self.slot(c, 1 - self.core)
        return self.copy(
            self.out.at[slot], slot, self.mate, self.fsend.at[c], self.frecv.at[c]
        )

    def order(self):
        return sorted(range(1, self.chips), key=lambda c: min(c, self.chips - c))

    def start(self):
        for c in self.order():
            self.first(c).start()
        self.first(0).start()

    def relay(self):
        for c in self.order():
            self.arrival(c).wait_recv()
            self.forward(c).start()

    def finish(self):
        for c in range(self.chips):
            self.first(c).wait_send()
        self.arrival(0).wait_recv()
        for c in range(1, self.chips):
            self.forwarded(c).wait_recv()
            self.forward(c).wait_send()


def gather_sems(n, count):
    return [pltpu.SemaphoreType.DMA((n // 2,))] * (4 * count)


def ag_kernel(n, count, *refs):
    srcs, outs = refs[:count], refs[count : 2 * count]
    sems, local = refs[2 * count : -1], refs[-1]
    greet(n)
    me = lax.axis_index("heads")
    gathers = [
        Gather(n, srcs[i], outs[i], *sems[4 * i : 4 * i + 4]) for i in range(count)
    ]
    owns = [
        pltpu.make_async_copy(srcs[i], outs[i].at[me], local.at[i]) for i in range(count)
    ]
    for g in gathers:
        g.start()
    for own in owns:
        own.start()
    for g in gathers:
        g.relay()
    for g in gathers:
        g.finish()
    for own in owns:
        own.wait()


def all_gather(arrays, n, cid):
    count = len(arrays)
    return pl.pallas_call(
        functools.partial(ag_kernel, n, count),
        out_shape=[jax.ShapeDtypeStruct((n,) + a.shape, a.dtype) for a in arrays],
        in_specs=[pl.BlockSpec(memory_space=pltpu.VMEM)] * count,
        out_specs=[pl.BlockSpec(memory_space=pltpu.VMEM)] * count,
        scratch_shapes=gather_sems(n, count) + [pltpu.SemaphoreType.DMA((count,))],
        compiler_params=pltpu.CompilerParams(
            collective_id=cid, has_side_effects=True, vmem_limit_bytes=VMEM_LIMIT
        ),
        name=f"gather_{cid}",
    )(*arrays)


def lookup_kernel(
    n, vocab, ids, table, whole, parts, part_out, whole_out, parts_out, acc,
    s0, s1, s2, s3, psend, precv, local
):
    step = pl.program_id(0)
    steps = pl.num_programs(0)
    me = lax.axis_index("heads")
    gather = Gather(n, whole, whole_out, s0, s1, s2, s3)

    def exchange(d):
        dst = lax.rem(me + d, n)
        return pltpu.make_async_remote_copy(
            src_ref=parts.at[dst],
            dst_ref=parts_out.at[me],
            send_sem=psend.at[d],
            recv_sem=precv.at[d],
            device_id={"heads": dst},
            device_id_type=MESH,
        )

    def came(d):
        src = lax.rem(me + n - d, n)
        return pltpu.make_async_remote_copy(
            src_ref=parts.at[src],
            dst_ref=parts_out.at[src],
            send_sem=psend.at[d],
            recv_sem=precv.at[d],
            device_id={"heads": src},
            device_id_type=MESH,
        )

    own_whole = pltpu.make_async_copy(whole, whole_out.at[me], local.at[0])
    own_part = pltpu.make_async_copy(parts.at[me], parts_out.at[me], local.at[1])

    @pl.when(step == 0)
    def _():
        greet(n)
        gather.start()
        for d in range(1, n):
            exchange(d).start()
        own_whole.start()
        own_part.start()
        acc[...] = jnp.zeros_like(acc)

    base = step * CHUNK
    rows = lax.broadcasted_iota(jnp.int32, (CHUNK, ids.shape[1]), 0) + base
    hot = jnp.where(rows == ids[...], 1.0, 0.0).astype(jnp.bfloat16)

    @pl.when(step < steps - 1)
    def _():
        acc[...] += jnp.dot(table[...], hot, preferred_element_type=jnp.float32)

    @pl.when(step == steps - 1)
    def _():
        columns = lax.broadcasted_iota(jnp.int32, table.shape, 1) + base
        block = jnp.where(columns < vocab, table[...].astype(jnp.float32), 0.0)
        total = acc[...] + jnp.dot(
            block.astype(jnp.bfloat16), hot, preferred_element_type=jnp.float32
        )
        part_out[...] = total.astype(jnp.bfloat16)
        gather.relay()
        gather.finish()
        for d in range(1, n):
            exchange(d).wait_send()
            came(d).wait_recv()
        own_whole.wait()
        own_part.wait()


def lookup(ids, table, whole, parts, n):
    cols, vocab = table.shape
    tokens = ids.shape[1]
    anywhere = pl.BlockSpec(memory_space=pl.ANY)
    return pl.pallas_call(
        functools.partial(lookup_kernel, n, vocab),
        grid=(pl.cdiv(vocab, CHUNK),),
        out_shape=[
            jax.ShapeDtypeStruct((cols, tokens), jnp.bfloat16),
            jax.ShapeDtypeStruct((n,) + whole.shape, whole.dtype),
            jax.ShapeDtypeStruct(parts.shape, parts.dtype),
        ],
        in_specs=[
            pl.BlockSpec((1, tokens), lambda i: (0, 0)),
            pl.BlockSpec((cols, CHUNK), lambda i: (0, i)),
            anywhere,
            anywhere,
        ],
        out_specs=[pl.BlockSpec((cols, tokens), lambda i: (0, 0)), anywhere, anywhere],
        scratch_shapes=[pltpu.VMEM((cols, tokens), jnp.float32)]
        + gather_sems(n, 1)
        + [
            pltpu.SemaphoreType.DMA((n,)),
            pltpu.SemaphoreType.DMA((n,)),
            pltpu.SemaphoreType.DMA((2,)),
        ],
        compiler_params=pltpu.CompilerParams(
            collective_id=0,
            has_side_effects=True,
            vmem_limit_bytes=VMEM_LIMIT,
            dimension_semantics=("arbitrary",),
        ),
        name="lookup",
    )(ids, table, whole, parts)


def conv_rows(x, state, taps, draft):
    tokens, channels = x.shape
    x3 = x.reshape(tokens // draft, draft, channels)
    s3 = state.reshape(tokens // draft, draft, channels)
    at = lax.broadcasted_iota(jnp.int32, (1, draft, channels), 1)
    kernel = taps.shape[0] - 1
    acc = None
    for k in range(kernel):
        back = kernel - 1 - k
        seen = x3
        if back:
            seen = jnp.where(at >= back, pltpu.roll(x3, back, 1), pltpu.roll(s3, back, 1))
        term = seen * taps[k : k + 1, :][None]
        acc = term if acc is None else acc + term
    acc = (acc + taps[kernel : kernel + 1, :][None]).reshape(tokens, channels)
    return acc * (1.0 / (1.0 + jnp.exp(-acc)))


def mixer_kernel(
    draft, zx, dt, bc_t, bc_state_t, bc_taps, x_state, x_taps, heads3, accepted, gain, h0,
    u_t, ssq, h_new, c_ref, y_ref, keep_ref
):
    tokens = zx.shape[0]
    width = zx.shape[1] // 2
    states = bc_t.shape[0] // 2
    f32, bf16 = jnp.float32, jnp.bfloat16
    bc = jnp.transpose(bc_t[...].astype(f32))
    bc_state = jnp.transpose(bc_state_t[...].astype(f32))
    bcc = conv_rows(bc, bc_state, bc_taps[...], draft)
    b = bcc[:, :states].astype(bf16)
    c = bcc[:, states:].astype(bf16)
    c_ref[...] = c.astype(f32)
    zx_all = zx[...].astype(f32)
    xc = conv_rows(zx_all[:, width:], x_state[...].astype(f32), x_taps[...], draft)
    bias, rate, skip = heads3[0:1, 0:1], heads3[1:2, 0:1], heads3[2:3, 0:1]
    raw = dt[...] + bias
    step_row = jnp.maximum(raw, 0.0) + jnp.log1p(jnp.exp(-jnp.abs(raw)))
    row = lax.broadcasted_iota(jnp.int32, (tokens, tokens), 0)
    col = lax.broadcasted_iota(jnp.int32, (tokens, tokens), 1)
    same = (row // draft == col // draft) & (col <= row)
    eye = row == col
    steps_col = jnp.sum(jnp.where(eye, step_row, 0.0), axis=1, keepdims=True)
    sum_col = jnp.sum(jnp.where(same, step_row, 0.0), axis=1, keepdims=True)
    sum_row = jnp.sum(jnp.where(eye, sum_col, 0.0), axis=0, keepdims=True)
    spread = jnp.exp(jnp.where(same, (sum_row - sum_col) * rate, -1e30))
    scores = dot_nt(c, b) * spread
    xw = xc * steps_col
    y = jnp.dot(scores.astype(bf16), xw.astype(bf16), preferred_element_type=f32)

    at = lax.broadcasted_iota(jnp.int32, (tokens, 1), 0) % draft
    kept = accepted[...]
    seqs = tokens // draft
    last = jnp.where(at == kept - 1, sum_col, 0.0).reshape(seqs, draft, 1)
    last = jnp.broadcast_to(jnp.sum(last, axis=1, keepdims=True), (seqs, draft, 1))
    last = last.reshape(tokens, 1)
    coef = jnp.exp(jnp.where(at < kept, (sum_col - last) * rate, -1e30))
    keep_ref[...] = jnp.broadcast_to(jnp.exp(-last * rate), keep_ref.shape)
    xk_t = jnp.transpose(xw * coef).astype(bf16)
    lanes = 128
    in_group = lanes // draft
    group_row = lax.broadcasted_iota(jnp.int32, (lanes, states), 0) // draft
    for q in range(seqs):
        rows = slice(q * draft, (q + 1) * draft)
        g = q // in_group
        state = h0[q]
        y_ref[rows, :] = dot_nt(c_ref[rows, :].astype(bf16), state.astype(bf16))
        mine = jnp.where(
            group_row == q % in_group, b[g * lanes : (g + 1) * lanes].astype(f32), 0.0
        )
        added = jnp.dot(
            xk_t[:, g * lanes : (g + 1) * lanes],
            mine.astype(bf16),
            preferred_element_type=f32,
        )
        h_new[q] = keep_ref[q * draft : q * draft + 1, :] * state + added
    y = y + jnp.exp(-sum_col * rate) * y_ref[...] + skip * xc
    z = zx_all[:, :width]
    gated = y * (z * (1.0 / (1.0 + jnp.exp(-z))))
    u = gated * gain[...]
    u_t[...] = jnp.transpose(u).astype(bf16)
    gated_t = jnp.transpose(gated)
    ssq[...] = jnp.broadcast_to(jnp.sum(gated_t * gated_t, axis=0, keepdims=True), ssq.shape)


def mix_tokens(draft, zx, h0, *rest):
    tokens, width = zx.shape[0], zx.shape[1] // 2
    states = h0.shape[2]
    count = 2 + len(rest)
    return pl.pallas_call(
        functools.partial(mixer_kernel, draft),
        out_shape=[
            jax.ShapeDtypeStruct((width, tokens), jnp.bfloat16),
            jax.ShapeDtypeStruct((8, tokens), jnp.float32),
            jax.ShapeDtypeStruct(h0.shape, jnp.float32),
        ],
        in_specs=[pl.BlockSpec(memory_space=pltpu.VMEM)] * count,
        out_specs=[pl.BlockSpec(memory_space=pltpu.VMEM)] * 3,
        scratch_shapes=[
            pltpu.VMEM((tokens, states), jnp.float32),
            pltpu.VMEM((tokens, width), jnp.float32),
            pltpu.VMEM((tokens, states), jnp.float32),
        ],
        compiler_params=pltpu.CompilerParams(vmem_limit_bytes=VMEM_LIMIT),
        name="mixer",
    )(zx, *rest, h0)


def local(
    draft_ids, accepted, embedding, norm_gain, w_zx, w_dt, w_bc, dt_bias, decay_rate,
    skip_weight, conv_x_w, conv_x_b, conv_bc_w, conv_bc_b, gate_gain, out_w, ssm_state,
    conv_x_state, conv_bc_state,
):
    f32, bf16 = jnp.float32, jnp.bfloat16
    n = lax.axis_size("heads")
    seqs, draft = draft_ids.shape
    tokens = seqs * draft
    width = w_zx.shape[3] // 2
    own_cols = embedding.shape[1]
    model = own_cols * n
    inner = width * n
    bc_here = w_bc.shape[2]
    kernel = conv_x_w.shape[1]
    me = lax.axis_index("heads")

    rows_before = draft - (kernel - 1)
    bc_pad = jnp.pad(conv_bc_state, ((0, 0), (0, 0), (rows_before, 0), (0, 0)))
    bc_pad = bc_pad.transpose(0, 3, 1, 2).reshape(LAYERS, bc_here, tokens)
    x_pad = jnp.pad(conv_x_state, ((0, 0), (0, 0), (rows_before, 0), (0, 0)))
    x_pad = x_pad.reshape(LAYERS, tokens, width)
    bc_taps = jnp.concatenate([conv_bc_w, conv_bc_b[:, None]], axis=1).transpose(0, 2, 1)
    bc_taps = jnp.pad(bc_taps, ((0, 0), (0, 0), (0, 128 - kernel - 1)))
    x_taps = jnp.concatenate([conv_x_w, conv_x_b[:, None]], axis=1).astype(f32)
    heads3 = jnp.stack([dt_bias, decay_rate, skip_weight], axis=1)
    kept = jnp.repeat(accepted, draft)[:, None]
    w_bd = jnp.concatenate([w_bc.transpose(0, 2, 1), w_dt.transpose(0, 2, 1)], axis=1)

    parts = out_w[1].reshape(width, n, own_cols).transpose(1, 0, 2)
    part, out_whole, out_mine = lookup(
        draft_ids.reshape(1, tokens), embedding.T, out_w[0], parts, n
    )
    stream, bc_pad_all, bc_taps_all = all_gather([part, bc_pad, bc_taps], n, 1)
    stream = stream.reshape(model, tokens)
    bc_pad_all = bc_pad_all.transpose(1, 0, 2, 3).reshape(LAYERS, n * bc_here, tokens)
    bc_taps_all = bc_taps_all[..., : kernel + 1].transpose(1, 3, 0, 2)
    bc_taps_all = bc_taps_all.reshape(LAYERS, kernel + 1, n * bc_here).astype(f32)
    saved_state, saved_x, saved_bc = [], [], []
    result = None
    for layer in range(LAYERS):
        value = stream.astype(f32)
        normed = (
            value
            * rms_scale(jnp.sum(value * value, 0, keepdims=True), model)
            * norm_gain[layer][:, None]
        ).astype(bf16)
        zx = dot_tn(normed, w_zx[layer].reshape(model, -1)).astype(bf16)
        bd = jnp.dot(w_bd[layer], normed, preferred_element_type=f32).astype(bf16)
        bc_t = bd[:bc_here]
        dt = bd[bc_here:].astype(f32)
        (bc_all,) = all_gather([bc_t], n, 2 + 2 * layer)
        u_t, ssq, h_new = mix_tokens(
            draft, zx, ssm_state[layer].reshape(seqs, width, -1), dt,
            bc_all.reshape(n * bc_here, tokens), bc_pad_all[layer], bc_taps_all[layer],
            x_pad[layer], x_taps[layer], heads3[layer], kept, gate_gain[layer][None],
        )
        saved_state.append(h_new.reshape(ssm_state.shape[1:]))
        window_x = jnp.concatenate(
            [conv_x_state[layer], zx[:, width:].reshape(seqs, draft, width)], axis=1
        )
        saved_x.append(keep_rows(window_x, accepted, kernel - 1))
        window_bc = jnp.concatenate(
            [conv_bc_state[layer], bc_t.T.reshape(seqs, draft, bc_here)], axis=1
        )
        saved_bc.append(keep_rows(window_bc, accepted, kernel - 1))
        u_all, ssq_all = all_gather([u_t, ssq], n, 3 + 2 * layer)
        u_all = u_all.reshape(inner, tokens)
        scale = rms_scale(jnp.sum(ssq_all[:, 0], axis=0), inner)[None]
        if layer + 1 < LAYERS:
            mix = dot_tn(out_whole.reshape(inner, model), u_all) * scale
            stream = (value + mix).astype(bf16)
        else:
            mix = dot_tn(out_mine.reshape(inner, own_cols), u_all) * scale
            mine = lax.dynamic_slice_in_dim(stream, me * own_cols, own_cols, 0)
            result = (mine.astype(f32) + mix).astype(bf16).T
    return (result, jnp.stack(saved_state), jnp.stack(saved_x), jnp.stack(saved_bc))


def solution(mesh):
    placed = (
        P("batch", None),
        P("batch"),
        P(None, "heads"),
        P(),
        P(None, None, "heads", None),
        P(None, None, "heads"),
        P(None, None, "heads"),
        P(None, "heads"),
        P(None, "heads"),
        P(None, "heads"),
        P(None, None, "heads"),
        P(None, "heads"),
        P(None, None, "heads"),
        P(None, "heads"),
        P(None, "heads"),
        P(None, "heads", None),
        P(None, "batch", "heads", None, None),
        P(None, "batch", None, "heads"),
        P(None, "batch", None, "heads"),
    )
    return jax.shard_map(
        local,
        mesh=mesh,
        in_specs=placed,
        out_specs=(
            P("batch", "heads"),
            P(None, "batch", "heads", None, None),
            P(None, "batch", None, "heads"),
            P(None, "batch", None, "heads"),
        ),
        check_vma=False,
    )
```

time: 374 us -> 183 us (0.49)
  Pallas kernels: 0 us -> 130 us
  waiting for transfers between devices: 110 us -> 0 us
  blocking collectives: 74.6 us -> 0 us
  other arithmetic: 75.7 us -> 11.9 us
  local copies, waits for them, and re-layouts: 81.7 us -> 27.6 us
  between operations: 15.4 us -> 0.95 us
  matrix products: 14.1 us -> 10.3 us
    pallas_call x0 -> x8, Pallas kernels: none -> 130 us  [the longest x5 77.5 us: all_gather(): pl.pallas_call(functools.partial(ag_kernel, n, count), out_shape=[jax.Sha...]
    psum x1 -> x0, waiting for transfers between devices: 85.9 us -> none  [local(): total = lax.psum(term, 'heads')]
    unnamed x181 -> x28, local copies, waits for them, and re-layouts: 55.4 us -> 4.05 us
    all_gather x3 -> x0, blocking collectives: 43.9 us -> none  [the longest x1 16.7 us: local(): lax.all_gather(conv_bc_state, 'heads', axis=3, tiled=True)]
    psum x2 -> x0, blocking collectives: 30.7 us -> none  [token_scale(): return rms_scale(lax.psum(local_sq, 'heads'), inner)]
    select_n x5 -> x0, other arithmetic: 18.6 us -> none  [the longest x2 17.3 us: recur(): kept = jnp.where((accepted == t + 1)[:, None, None], state, kept)]
    unnamed x5 -> x0, waiting for transfers between devices: 16.4 us -> none
    reduce_sum x8 -> x3, other arithmetic: 14.4 us -> 3.88 us  [the longest x1 2.04 us: local(): jnp.sum(value * value, 0, keepdims=True)]
  transfers between devices with their start and end apart: 4 -> 0, of which waited for: 3 -> 0; matrix products, arithmetic and copies ran while one was open for 13% -> 0% of each run, Pallas kernels for 0% -> 0%
where the time goes in v1:
time: 183 us; the launch traced here: 181 us
  Pallas kernels  130 us (71%)
  local copies, waits for them, and re-layouts  27.6 us (15%)
  other arithmetic  11.9 us (7%)
  matrix products  10.3 us (6%)
    pallas_call x5, Pallas kernels, all_gather(): pl.pallas_call(functools.partial(ag_kernel, n, count), out_shape=[jax.Sha...  77.5 us
    pallas_call x1, Pallas kernels, lookup(): pl.pallas_call(functools.partial(lookup_kernel, n, vocab), grid=(pl.cdiv(...  43.1 us
    pallas_call x2, Pallas kernels, mix_tokens(): pl.pallas_call(functools.partial(mixer_kernel, draft), out_shape=[jax.Sha...  9.68 us
    dot_general x4, matrix products, dot_tn(): lax.dot_general(a, b, (((0,), (0,)), ((), ())), preferred_element_type=jn...  9.23 us
    unnamed x28, local copies, waits for them, and re-layouts  4.05 us
    another operation x1, local copies, waits for them, and re-layouts, local(): ssm_state[layer].reshape(seqs, width, -1)  3.96 us

profile of v1, /device:TPU:0, one launch (start us, length us, event | category | flops | bytes accessed | tf_op | source)
XLA Modules:
  0.0 181.1 jit_solution(2036383227433802943)
XLA Ops:
  0.6 0.7 copy.161
  1.4 1.3 fusion.59
  2.7 0.7 pad_maximum_fusion.7
  3.5 0.6 copy_bitcast_fusion.3
  4.0 0.7 broadcast_compare_fusion.6
  4.7 0.7 maximum_convert_fusion
  5.4 0.6 slice_bitcast_fusion.7
  6.0 0.8 copy.154
  6.8 0.8 copy.155
  7.6 0.6 pad.13.refs_2_
  8.2 0.7 copy.158
  9.0 0.8 copy.151
  9.7 0.7 reshape.112.ids
  10.4 0.7 broadcast_in_dim.161
  11.1 0.9 slice_reduce_fusion.2
  12.1 0.8 fusion.57
  12.8 0.1 copy.197
  13.0 0.8 slice_bitcast_fusion.6
  13.8 0.8 pad_bitcast_fusion
  14.6 0.2 copy.153
  14.8 0.7 copy.156.refs_1_
  15.6 0.8 broadcast_in_dim_reshape.4.accepted
  16.4 0.8 pad_slice_fusion.2
  17.2 0.7 copy_bitcast_fusion.1
  17.9 0.8 fusion.54
  18.7 0.3 reshape_squeeze.15
  19.0 0.8 copy.204
  19.8 43.1 %lookup.1 = (bf16[320,384]{1,0:T(8,128)(2,1)}, bf16[8,64,2560]{2,1,0:T(8,128)(2,1)}, bf16[8,64,320]{2,1,0:T(8,128)(2,1)}) custom-call(s32[1,384]{1,0:T(1,128)} %reshape.112.ids, bf16[320,50280]{1,0:T(8,128)(2,1)} %bitcast.114, bf16[64,2560]{1,0:T(8,128)(2,1)} %get-tuple-element.57.whole, bf16[8,64,320]{2,1,0:T(8,128)(2,1)} %bitcast.121), custom_call_target="tpu_custom_call" | custom-call | tf_op jit(solution)/shard_map/lookup/pallas_call | solution.py:233
  62.9 36.3 %gather_1.1 = (bf16[8,320,384]{2,1,0:T(8,128)(2,1)}, bf16[8,2,32,384]{3,2,1,0:T(8,128)(2,1)}, bf16[8,2,32,128]{3,2,1,0:T(8,128)(2,1)}) custom-call(bf16[320,384]{1,0:T(8,128)(2,1)} %get-tuple-element.20.refs_0_, bf16[2,32,384]{2,1,0:T(8,128)(2,1)} %copy.156.refs_1_, bf16[2,32,128]{2,1,0:T(8,128)(2,1)} %pad.13.refs_2_), custom_call_target="tpu_custom_call" | custom-call | tf_op jit(solution)/shard_map/gather_1/pallas_call | solution.py:147
  99.2 2.0 %fusion.55 = (bf16[1,8,32,384]{3,2,0,1:T(8,128)(2,1)}, bf16[1,8,32,384]{3,2,0,1:T(8,128)(2,1)}) fusion(bf16[2,8,32,384]{3,2,0,1:T(8,128)(2,1)} %bitcast.131), kind=kLoop, calls=%fused_computation.113 | loop fusion | bytes 786432 | tf_op jit(solution)/shard_map/slice | solution.py:426
  101.2 2.0 %multiply_reduce_fusion = f32[384]{0:T(512)S(1)} fusion(bf16[8,320,384]{2,1,0:T(8,128)(2,1)} %get-tuple-element.21), kind=kLoop, calls=%fused_computation.10 | loop fusion | flops 2948736 | bytes 1967616 | tf_op jit(solution)/shard_map/reduce_sum | solution.py:416
  103.3 0.7 copy.194.bc_taps
  104.0 0.7 copy.193.bc_taps
  104.7 0.5 multiply_convert_fusion
  105.2 0.4 copy-done.6
  105.6 0.4 convolution_convert_fusion.3
  106.0 0.5 copy-done.8
  106.5 0.7 convolution_convert_fusion.1.zx
  107.3 0.6 slice_convert_fusion.1.dt
  107.9 0.6 slice_bitcast_fusion.10
  108.5 0.1 copy.185
  108.6 0.6 fusion.35
  109.3 0.1 fusion.50
  109.4 8.4 %gather_2.1 = bf16[8,32,384]{2,1,0:T(8,128)(2,1)} custom-call(bf16[32,384]{1,0:T(8,128)(2,1)} %get-tuple-element.69.refs_0_), custom_call_target="tpu_custom_call" | custom-call | tf_op jit(solution)/shard_map/gather_2/pallas_call | solution.py:147
  117.8 4.0 %slice_bitcast_fusion = (f32[48,64,128]{2,1,0:T(8,128)}, f32[48,64,128]{2,1,0:T(8,128)}) fusion(f32[2,48,1,64,128]{4,3,1,2,0:T(8,128)} %bitcast.118), kind=kLoop, calls=%fused_computation.12 | loop fusion | bytes 6291456 | tf_op jit(solution)/shard_map/reshape;squeeze | solution.py:425
  121.8 4.8 %mixer.2 = (bf16[64,384]{1,0:T(8,128)(2,1)}, f32[8,384]{1,0:T(8,128)}, f32[48,64,128]{2,1,0:T(8,128)}) custom-call(bf16[384,128]{1,0:T(8,128)(2,1)} %copy-done.4, f32[1,384]{1,0:T(1,128)} %slice_convert_fusion.1.dt, bf16[256,384]{1,0:T(8,128)(2,1)} %bitcast.124, bf16[256,384]{1,0:T(8,128)(2,1)} %bitcast.127, f32[5,256]{1,0:T(8,128)} %copy.193.bc_taps, ...), custom_call_target="tpu_custom_call" | custom-call | tf_op jit(solution)/shard_map/mixer/pallas_call | solution.py:353
  126.5 12.3 %gather_3.1 = (bf16[8,64,384]{2,1,0:T(8,128)(2,1)}, f32[8,8,384]{2,1,0:T(8,128)}) custom-call(bf16[64,384]{1,0:T(8,128)(2,1)} %get-tuple-element.25.refs_0_, f32[8,384]{1,0:T(8,128)} %get-tuple-element.26.refs_1_), custom_call_target="tpu_custom_call" | custom-call | tf_op jit(solution)/shard_map/gather_3/pallas_call | solution.py:147
  138.8 0.9 slice_reduce_fusion.1
  139.7 3.5 %fusion.3 = (f32[384]{0:T(512)S(1)}, bf16[2560,384]{1,0:T(8,128)(2,1)S(1)}) fusion(f32[384]{0:T(512)S(1)} %add_rsqrt_fusion.2, bf16[8,64,2560]{2,1,0:T(8,128)(2,1)} %get-tuple-element.22, bf16[8,64,384]{2,1,0:T(8,128)(2,1)} %get-tuple-element.27, bf16[2560,384]{1,0:T(8,128)(2,1)S(1)} %bitcast.115), kind=kOutput, calls=%fused_computation.6 | convolution fusion | flops 1013513856 | bytes 6949888 | tf_op jit(solution)/shard_map/dot_general | solution.py:22
  143.3 0.7 convolution_convert_fusion.2
  144.0 0.6 slice_convert_fusion.dt
  144.6 0.6 slice_bitcast_fusion.9
  145.2 0.1 copy.187
  145.3 0.6 fusion.28
  146.0 0.7 copy.190
  146.7 2.8 %convolution_convert_fusion.zx = bf16[384,128]{1,0:T(8,128)(2,1)S(1)} fusion(bf16[2,2560,1,128]{3,1,2,0:T(8,128)(2,1)S(1)} %copy-done.9, bf16[2560,384]{1,0:T(8,128)(2,1)} %copy-done.10, f32[2560]{0:T(1024)S(1)} %get-tuple-element.52, f32[384]{0:T(512)S(1)} %add_rsqrt_fusion.1), kind=kOutput, calls=%fused_computation.19 | convolution fusion | flops 255639552 | bytes 2734080 | tf_op jit(solution)/shard_map/dot_general | solution.py:22
  149.6 0.1 fusion.51
  149.7 0.7 pad_maximum_fusion.2
  150.4 8.3 %gather_4.1 = bf16[8,32,384]{2,1,0:T(8,128)(2,1)} custom-call(bf16[32,384]{1,0:T(8,128)(2,1)} %get-tuple-element.71.refs_0_), custom_call_target="tpu_custom_call" | custom-call | tf_op jit(solution)/shard_map/gather_4/pallas_call | solution.py:147
  158.7 4.9 %mixer.3 = (bf16[64,384]{1,0:T(8,128)(2,1)}, f32[8,384]{1,0:T(8,128)}, f32[48,64,128]{2,1,0:T(8,128)}) custom-call(bf16[384,128]{1,0:T(8,128)(2,1)} %copy-done.5, f32[1,384]{1,0:T(1,128)} %slice_convert_fusion.dt, bf16[256,384]{1,0:T(8,128)(2,1)} %bitcast.125, bf16[256,384]{1,0:T(8,128)(2,1)} %bitcast.126, f32[5,256]{1,0:T(8,128)} %copy.194.bc_taps, ...), custom_call_target="tpu_custom_call" | custom-call | tf_op jit(solution)/shard_map/mixer/pallas_call | solution.py:353
  163.6 12.2 %gather_5.1 = (bf16[8,64,384]{2,1,0:T(8,128)(2,1)}, f32[8,8,384]{2,1,0:T(8,128)}) custom-call(bf16[64,384]{1,0:T(8,128)(2,1)} %get-tuple-element.30.refs_0_, f32[8,384]{1,0:T(8,128)} %get-tuple-element.31.refs_1_), custom_call_target="tpu_custom_call" | custom-call | tf_op jit(solution)/shard_map/gather_5/pallas_call | solution.py:147
  175.9 0.9 slice_reduce_fusion
  176.8 2.2 %fusion.9 = bf16[384,320]{0,1:T(8,128)(2,1)} fusion(bf16[8,64,320]{2,1,0:T(8,128)(2,1)} %get-tuple-element.29, bf16[8,64,384]{2,1,0:T(8,128)(2,1)} %get-tuple-element.32, f32[384]{0:T(512)S(1)} %add_rsqrt_fusion, bf16[2560,384]{1,0:T(8,128)(2,1)} %copy-done.10, s32[]{:T(128)S(6)} %select_n.89), kind=kOutput, calls=%fused_computation.18 | convolution fusion | flops 126320640 | bytes 1213956 | tf_op jit(solution)/shard_map/dot_general | solution.py:22
  179.1 2.1 %maximum_bitcast_fusion = f32[2,48,1,64,128]{4,3,2,1,0:T(8,128)} fusion(f32[1,48,1,64,128]{4,3,1,2,0:T(8,128)S(1)} %bitcast.123, f32[1,48,1,64,128]{4,3,1,2,0:T(8,128)S(1)} %bitcast.122), kind=kLoop, calls=%fused_computation.11 | loop fusion | flops 786432 | bytes 6291456
  (35 shorter events, 0.8 us)
Async XLA Ops:
  0.6 17.3 %copy-start.3 = (bf16[2,64,2560]{2,1,0:T(8,128)(2,1)S(1)}, bf16[2,64,2560]{2,1,0:T(8,128)(2,1)}, u32[]{:S(2)}) copy-start(bf16[2,64,2560]{2,1,0:T(8,128)(2,1)} %param.34) | copy-start | bytes 1966084
  99.2 4.0 %copy-start.7 = (bf16[8,2,32,128]{3,2,1,0:T(8,128)(2,1)S(1)}, bf16[8,2,32,128]{3,2,1,0:T(8,128)(2,1)}, u32[]{:S(2)}) copy-start(bf16[8,2,32,128]{3,2,1,0:T(8,128)(2,1)} %get-tuple-element.24) | copy-start | bytes 393220
  99.2 5.4 %copy-start = (bf16[8,320,384]{2,1,0:T(8,128)(2,1)S(1)}, bf16[8,320,384]{2,1,0:T(8,128)(2,1)}, u32[]{:S(2)}) copy-start(bf16[8,320,384]{2,1,0:T(8,128)(2,1)} %get-tuple-element.21) | copy-start | bytes 5898244
  104.7 1.0 copy-start.6
  105.2 1.3 copy-start.8
  107.3 14.5 %copy-start.4 = (bf16[384,128]{1,0:T(8,128)(2,1)}, bf16[384,128]{1,0:T(8,128)(2,1)S(1)}, u32[]{:S(2)}) copy-start(bf16[384,128]{1,0:T(8,128)(2,1)S(1)} %convolution_convert_fusion.1.zx) | copy-start | bytes 294916
  143.2 2.0 %copy-start.10 = (bf16[2560,384]{1,0:T(8,128)(2,1)}, bf16[2560,384]{1,0:T(8,128)(2,1)S(1)}, u32[]{:S(2)}) copy-start(bf16[2560,384]{1,0:T(8,128)(2,1)S(1)} %get-tuple-element.86) | copy-start | bytes 5898244
  143.3 3.5 %copy-start.9 = (bf16[2,2560,1,128]{3,1,2,0:T(8,128)(2,1)S(1)}, bf16[2,2560,1,128]{3,1,2,0:T(8,128)(2,1)}, u32[]{:S(2)}) copy-start(bf16[2,2560,1,128]{3,1,2,0:T(8,128)(2,1)} %param.23) | copy-start | bytes 3932164
  149.5 9.2 %copy-start.5 = (bf16[384,128]{1,0:T(8,128)(2,1)}, bf16[384,128]{1,0:T(8,128)(2,1)S(1)}, u32[]{:S(2)}) copy-start(bf16[384,128]{1,0:T(8,128)(2,1)S(1)} %convolution_convert_fusion.zx) | copy-start | bytes 294916
  158.7 20.3 %copy-start.1 = (f32[48,64,128]{2,1,0:T(8,128)S(1)}, f32[48,64,128]{2,1,0:T(8,128)}, u32[]{:S(2)}) copy-start(f32[48,64,128]{2,1,0:T(8,128)} %get-tuple-element.34) | copy-start | bytes 4718596
  163.6 15.4 %copy-start.2 = (f32[48,64,128]{2,1,0:T(8,128)S(1)}, f32[48,64,128]{2,1,0:T(8,128)}, u32[]{:S(2)}) copy-start(f32[48,64,128]{2,1,0:T(8,128)} %get-tuple-element.35) | copy-start | bytes 4718596

commit v2 on v1

--- a/solution.py
+++ b/solution.py
@@ -56,9 +56,6 @@
         self.chips = n // 2
         self.mate = self.me + 1 - 2 * self.core
 
-    def slot(self, c, core):
-        return 2 * lax.rem(self.chip + self.chips - c, self.chips) + core
-
     def copy(self, src, slot, device, send, recv):
         return pltpu.make_async_remote_copy(
             src_ref=src,
@@ -69,54 +66,78 @@
             device_id_type=MESH,
         )
 
-    def first(self, c):
-        if c == 0:
-            return self.copy(self.src, self.me, self.mate, self.send.at[0], self.recv.at[0])
-        dst = 2 * lax.rem(self.chip + c, self.chips) + self.core
-        return self.copy(self.src, self.me, dst, self.send.at[c], self.recv.at[c])
-
-    def arrival(self, c):
-        if c == 0:
-            return self.copy(self.src, self.mate, self.mate, self.send.at[0], self.recv.at[0])
-        slot = self.slot(c, self.core)
-        return self.copy(self.src, slot, slot, self.send.at[c], self.recv.at[c])
-
-    def forward(self, c):
-        slot = self.slot(c, self.core)
+    def index(self, side, c):
+        return c if side < 0 else self.chips - 1 + c
+
+    def has(self, side, c):
+        return self.chip >= c if side < 0 else self.chip + c < self.chips
+
+    def slot(self, side, c, core):
+        return 2 * (self.chip + side * c) + core
+
+    def hop(self, side, c):
+        i = self.index(side, c + 1)
+        slot = self.me if c == 0 else self.slot(side, c, self.core)
+        src = self.src if c == 0 else self.out.at[slot]
+        return self.copy(src, slot, self.slot(-side, 1, self.core), self.send.at[i], self.recv.at[i])
+
+    def arrival(self, side, c):
+        i = self.index(side, c)
+        slot = self.slot(side, c, self.core)
         return self.copy(
-            self.out.at[slot], slot, self.mate, self.fsend.at[c], self.frecv.at[c]
-        )
-
-    def forwarded(self, c):
-        slot = self.slot(c, 1 - self.core)
-        return self.copy(
-            self.out.at[slot], slot, self.mate, self.fsend.at[c], self.frecv.at[c]
-        )
-
-    def order(self):
-        return sorted(range(1, self.chips), key=lambda c: min(c, self.chips - c))
+            self.src, slot, self.slot(side, 1, self.core), self.send.at[i], self.recv.at[i]
+        )
+
+    def across(self, side, c, core):
+        i = self.index(side, c)
+        slot = self.slot(side, c, core)
+        return self.copy(self.out.at[slot], slot, self.mate, self.fsend.at[i], self.frecv.at[i])
+
+    def first(self, slot):
+        return self.copy(self.src, slot, self.mate, self.send.at[0], self.recv.at[0])
+
+    def places(self):
+        return [(side, c) for c in range(1, self.chips) for side in (-1, 1)]
 
     def start(self):
-        for c in self.order():
-            self.first(c).start()
-        self.first(0).start()
+        for side in (-1, 1):
+            pl.when(self.has(-side, 1))(lambda side=side: self.hop(side, 0).start())
+        self.first(self.me).start()
 
     def relay(self):
-        for c in self.order():
-            self.arrival(c).wait_recv()
-            self.forward(c).start()
+        for side, c in self.places():
+
+            @pl.when(self.has(side, c))
+            def _():
+                self.arrival(side, c).wait_recv()
+
+            @pl.when(self.has(side, c) & self.has(-side, 1))
+            def _():
+                self.hop(side, c).start()
+
+            @pl.when(self.has(side, c))
+            def _():
+                self.across(side, c, self.core).start()
 
     def finish(self):
-        for c in range(self.chips):
-            self.first(c).wait_send()
-        self.arrival(0).wait_recv()
-        for c in range(1, self.chips):
-            self.forwarded(c).wait_recv()
-            self.forward(c).wait_send()
+        self.first(self.me).wait_send()
+        self.first(self.mate).wait_recv()
+        for side in (-1, 1):
+            pl.when(self.has(-side, 1))(lambda side=side: self.hop(side, 0).wait_send())
+        for side, c in self.places():
+
+            @pl.when(self.has(side, c) & self.has(-side, 1))
+            def _():
+                self.hop(side, c).wait_send()
+
+            @pl.when(self.has(side, c))
+            def _():
+                self.across(side, c, 1 - self.core).wait_recv()
+                self.across(side, c, self.core).wait_send()
 
 
 def gather_sems(n, count):
-    return [pltpu.SemaphoreType.DMA((n // 2,))] * (4 * count)
+    return [pltpu.SemaphoreType.DMA((n,))] * (4 * count)
 
 
 def ag_kernel(n, count, *refs):

time: 183 us -> 206 us (1.13)
  Pallas kernels: 130 us -> 153 us
    pallas_call x1, Pallas kernels: 43.1 us -> 55.4 us  [lookup(): pl.pallas_call(functools.partial(lookup_kernel, n, vocab), grid=(pl.cdiv(...]
    pallas_call x5, Pallas kernels: 77.5 us -> 87.8 us  [all_gather(): pl.pallas_call(functools.partial(ag_kernel, n, count), out_shape=[jax.Sha...]
where the time goes in v2:
time: 206 us; the launch traced here: 204 us
  Pallas kernels  153 us (74%)
  local copies, waits for them, and re-layouts  27.6 us (13%)
  other arithmetic  12.1 us (6%)
  matrix products  10.3 us (5%)
    pallas_call x5, Pallas kernels, all_gather(): pl.pallas_call(functools.partial(ag_kernel, n, count), out_shape=[jax.Sha...  87.8 us
    pallas_call x1, Pallas kernels, lookup(): pl.pallas_call(functools.partial(lookup_kernel, n, vocab), grid=(pl.cdiv(...  55.4 us
    pallas_call x2, Pallas kernels, mix_tokens(): pl.pallas_call(functools.partial(mixer_kernel, draft), out_shape=[jax.Sha...  9.68 us
    dot_general x4, matrix products, dot_tn(): lax.dot_general(a, b, (((0,), (0,)), ((), ())), preferred_element_type=jn...  9.22 us

profile of v2, /device:TPU:0, one launch (start us, length us, event | category | flops | bytes accessed | tf_op | source)
XLA Modules:
  0.0 203.8 jit_solution(15277485531464628808)
XLA Ops:
  0.6 0.7 copy.161
  1.4 1.3 fusion.59
  2.7 0.7 pad_maximum_fusion.7
  3.5 0.6 copy_bitcast_fusion.3
  4.0 0.7 broadcast_compare_fusion.6
  4.7 0.7 maximum_convert_fusion
  5.4 0.6 slice_bitcast_fusion.7
  6.0 0.8 copy.154
  6.8 0.8 copy.155
  7.6 0.6 pad.13.refs_2_
  8.2 0.7 copy.158
  9.0 0.8 copy.151
  9.7 0.7 reshape.112.ids
  10.4 0.7 broadcast_in_dim.161
  11.1 0.9 slice_reduce_fusion.2
  12.1 0.8 fusion.57
  12.8 0.1 copy.197
  13.0 0.8 slice_bitcast_fusion.6
  13.8 0.8 pad_bitcast_fusion
  14.6 0.2 copy.153
  14.8 0.7 copy.156.refs_1_
  15.6 0.8 broadcast_in_dim_reshape.4.accepted
  16.4 0.8 pad_slice_fusion.2
  17.2 0.7 copy_bitcast_fusion.1
  17.9 0.8 fusion.54
  18.7 0.3 reshape_squeeze.15
  19.0 0.8 copy.204
  19.8 55.4 %lookup.1 = (bf16[320,384]{1,0:T(8,128)(2,1)}, bf16[8,64,2560]{2,1,0:T(8,128)(2,1)}, bf16[8,64,320]{2,1,0:T(8,128)(2,1)}) custom-call(s32[1,384]{1,0:T(1,128)} %reshape.112.ids, bf16[320,50280]{1,0:T(8,128)(2,1)} %bitcast.114, bf16[64,2560]{1,0:T(8,128)(2,1)} %get-tuple-element.57.whole, bf16[8,64,320]{2,1,0:T(8,128)(2,1)} %bitcast.121), custom_call_target="tpu_custom_call" | custom-call | tf_op jit(solution)/shard_map/lookup/pallas_call | solution.py:254
  75.1 28.7 %gather_1.1 = (bf16[8,320,384]{2,1,0:T(8,128)(2,1)}, bf16[8,2,32,384]{3,2,1,0:T(8,128)(2,1)}, bf16[8,2,32,128]{3,2,1,0:T(8,128)(2,1)}) custom-call(bf16[320,384]{1,0:T(8,128)(2,1)} %get-tuple-element.20.refs_0_, bf16[2,32,384]{2,1,0:T(8,128)(2,1)} %copy.156.refs_1_, bf16[2,32,128]{2,1,0:T(8,128)(2,1)} %pad.13.refs_2_), custom_call_target="tpu_custom_call" | custom-call | tf_op jit(solution)/shard_map/gather_1/pallas_call | solution.py:168
  103.9 2.0 fusion.55
  105.8 2.0 %multiply_reduce_fusion = f32[384]{0:T(512)S(1)} fusion(bf16[8,320,384]{2,1,0:T(8,128)(2,1)} %get-tuple-element.21), kind=kLoop, calls=%fused_computation.10 | loop fusion | flops 2948736 | bytes 1967616 | tf_op jit(solution)/shard_map/reduce_sum | solution.py:437
  108.0 0.7 copy.194.bc_taps
  108.6 0.7 copy.193.bc_taps
  109.3 0.5 multiply_convert_fusion
  109.9 0.4 copy-done.6
  110.3 0.4 convolution_convert_fusion.3
  110.7 0.5 copy-done.8
  111.2 0.7 convolution_convert_fusion.1.zx
  111.9 0.6 slice_convert_fusion.1.dt
  112.5 0.6 slice_bitcast_fusion.10
  113.1 0.1 copy.185
  113.2 0.6 fusion.35
  113.9 0.1 fusion.50
  114.1 12.9 %gather_2.1 = bf16[8,32,384]{2,1,0:T(8,128)(2,1)} custom-call(bf16[32,384]{1,0:T(8,128)(2,1)} %get-tuple-element.69.refs_0_), custom_call_target="tpu_custom_call" | custom-call | tf_op jit(solution)/shard_map/gather_2/pallas_call | solution.py:168
  127.0 4.0 %slice_bitcast_fusion = (f32[48,64,128]{2,1,0:T(8,128)}, f32[48,64,128]{2,1,0:T(8,128)}) fusion(f32[2,48,1,64,128]{4,3,1,2,0:T(8,128)} %bitcast.118), kind=kLoop, calls=%fused_computation.12 | loop fusion | bytes 6291456 | tf_op jit(solution)/shard_map/reshape;squeeze | solution.py:446
  131.0 4.8 %mixer.2 = (bf16[64,384]{1,0:T(8,128)(2,1)}, f32[8,384]{1,0:T(8,128)}, f32[48,64,128]{2,1,0:T(8,128)}) custom-call(bf16[384,128]{1,0:T(8,128)(2,1)} %copy-done.4, f32[1,384]{1,0:T(1,128)} %slice_convert_fusion.1.dt, bf16[256,384]{1,0:T(8,128)(2,1)} %bitcast.124, bf16[256,384]{1,0:T(8,128)(2,1)} %bitcast.127, f32[5,256]{1,0:T(8,128)} %copy.193.bc_taps, ...), custom_call_target="tpu_custom_call" | custom-call | tf_op jit(solution)/shard_map/mixer/pallas_call | solution.py:374
  135.8 17.1 %gather_3.1 = (bf16[8,64,384]{2,1,0:T(8,128)(2,1)}, f32[8,8,384]{2,1,0:T(8,128)}) custom-call(bf16[64,384]{1,0:T(8,128)(2,1)} %get-tuple-element.25.refs_0_, f32[8,384]{1,0:T(8,128)} %get-tuple-element.26.refs_1_), custom_call_target="tpu_custom_call" | custom-call | tf_op jit(solution)/shard_map/gather_3/pallas_call | solution.py:168
  152.9 0.9 slice_reduce_fusion.1
  153.8 3.5 %fusion.3 = (f32[384]{0:T(512)S(1)}, bf16[2560,384]{1,0:T(8,128)(2,1)S(1)}) fusion(f32[384]{0:T(512)S(1)} %add_rsqrt_fusion.2, bf16[8,64,2560]{2,1,0:T(8,128)(2,1)} %get-tuple-element.22, bf16[8,64,384]{2,1,0:T(8,128)(2,1)} %get-tuple-element.27, bf16[2560,384]{1,0:T(8,128)(2,1)S(1)} %bitcast.115), kind=kOutput, calls=%fused_computation.6 | convolution fusion | flops 1013513856 | bytes 6949888 | tf_op jit(solution)/shard_map/dot_general | solution.py:22
  157.3 0.7 convolution_convert_fusion.2
  158.0 0.6 slice_convert_fusion.dt
  158.6 0.6 slice_bitcast_fusion.9
  159.2 0.1 copy.187
  159.4 0.7 fusion.28
  160.2 0.7 copy.190
  160.9 2.8 %convolution_convert_fusion.zx = bf16[384,128]{1,0:T(8,128)(2,1)S(1)} fusion(bf16[2,2560,1,128]{3,1,2,0:T(8,128)(2,1)S(1)} %copy-done.9, bf16[2560,384]{1,0:T(8,128)(2,1)} %copy-done.10, f32[2560]{0:T(1024)S(1)} %get-tuple-element.52, f32[384]{0:T(512)S(1)} %add_rsqrt_fusion.1), kind=kOutput, calls=%fused_computation.19 | convolution fusion | flops 255639552 | bytes 2734080 | tf_op jit(solution)/shard_map/dot_general | solution.py:22
  163.8 0.1 fusion.51
  164.0 0.7 pad_maximum_fusion.2
  164.6 12.9 %gather_4.1 = bf16[8,32,384]{2,1,0:T(8,128)(2,1)} custom-call(bf16[32,384]{1,0:T(8,128)(2,1)} %get-tuple-element.71.refs_0_), custom_call_target="tpu_custom_call" | custom-call | tf_op jit(solution)/shard_map/gather_4/pallas_call | solution.py:168
  177.6 4.9 %mixer.3 = (bf16[64,384]{1,0:T(8,128)(2,1)}, f32[8,384]{1,0:T(8,128)}, f32[48,64,128]{2,1,0:T(8,128)}) custom-call(bf16[384,128]{1,0:T(8,128)(2,1)} %copy-done.5, f32[1,384]{1,0:T(1,128)} %slice_convert_fusion.dt, bf16[256,384]{1,0:T(8,128)(2,1)} %bitcast.125, bf16[256,384]{1,0:T(8,128)(2,1)} %bitcast.126, f32[5,256]{1,0:T(8,128)} %copy.194.bc_taps, ...), custom_call_target="tpu_custom_call" | custom-call | tf_op jit(solution)/shard_map/mixer/pallas_call | solution.py:374
  182.4 16.1 %gather_5.1 = (bf16[8,64,384]{2,1,0:T(8,128)(2,1)}, f32[8,8,384]{2,1,0:T(8,128)}) custom-call(bf16[64,384]{1,0:T(8,128)(2,1)} %get-tuple-element.30.refs_0_, f32[8,384]{1,0:T(8,128)} %get-tuple-element.31.refs_1_), custom_call_target="tpu_custom_call" | custom-call | tf_op jit(solution)/shard_map/gather_5/pallas_call | solution.py:168
  198.6 0.9 slice_reduce_fusion
  199.5 2.2 %fusion.9 = bf16[384,320]{0,1:T(8,128)(2,1)} fusion(bf16[8,64,320]{2,1,0:T(8,128)(2,1)} %get-tuple-element.29, bf16[8,64,384]{2,1,0:T(8,128)(2,1)} %get-tuple-element.32, f32[384]{0:T(512)S(1)} %add_rsqrt_fusion, bf16[2560,384]{1,0:T(8,128)(2,1)} %copy-done.10, s32[]{:T(128)S(6)} %select_n.89), kind=kOutput, calls=%fused_computation.18 | convolution fusion | flops 126320640 | bytes 1213956 | tf_op jit(solution)/shard_map/dot_general | solution.py:22
  201.7 2.1 %maximum_bitcast_fusion = f32[2,48,1,64,128]{4,3,2,1,0:T(8,128)} fusion(f32[1,48,1,64,128]{4,3,1,2,0:T(8,128)S(1)} %bitcast.123, f32[1,48,1,64,128]{4,3,1,2,0:T(8,128)S(1)} %bitcast.122), kind=kLoop, calls=%fused_computation.11 | loop fusion | flops 786432 | bytes 6291456
  (35 shorter events, 0.8 us)
Async XLA Ops:
  0.6 17.3 %copy-start.3 = (bf16[2,64,2560]{2,1,0:T(8,128)(2,1)S(1)}, bf16[2,64,2560]{2,1,0:T(8,128)(2,1)}, u32[]{:S(2)}) copy-start(bf16[2,64,2560]{2,1,0:T(8,128)(2,1)} %param.34) | copy-start | bytes 1966084
  103.9 4.0 %copy-start.7 = (bf16[8,2,32,128]{3,2,1,0:T(8,128)(2,1)S(1)}, bf16[8,2,32,128]{3,2,1,0:T(8,128)(2,1)}, u32[]{:S(2)}) copy-start(bf16[8,2,32,128]{3,2,1,0:T(8,128)(2,1)} %get-tuple-element.24) | copy-start | bytes 393220
  103.9 5.4 %copy-start = (bf16[8,320,384]{2,1,0:T(8,128)(2,1)S(1)}, bf16[8,320,384]{2,1,0:T(8,128)(2,1)}, u32[]{:S(2)}) copy-start(bf16[8,320,384]{2,1,0:T(8,128)(2,1)} %get-tuple-element.21) | copy-start | bytes 5898244
  109.3 1.0 copy-start.6
  109.8 1.3 copy-start.8
  111.9 19.0 %copy-start.4 = (bf16[384,128]{1,0:T(8,128)(2,1)}, bf16[384,128]{1,0:T(8,128)(2,1)S(1)}, u32[]{:S(2)}) copy-start(bf16[384,128]{1,0:T(8,128)(2,1)S(1)} %convolution_convert_fusion.1.zx) | copy-start | bytes 294916
  157.3 2.0 copy-start.10
  157.3 3.6 %copy-start.9 = (bf16[2,2560,1,128]{3,1,2,0:T(8,128)(2,1)S(1)}, bf16[2,2560,1,128]{3,1,2,0:T(8,128)(2,1)}, u32[]{:S(2)}) copy-start(bf16[2,2560,1,128]{3,1,2,0:T(8,128)(2,1)} %param.23) | copy-start | bytes 3932164
  163.7 13.8 %copy-start.5 = (bf16[384,128]{1,0:T(8,128)(2,1)}, bf16[384,128]{1,0:T(8,128)(2,1)S(1)}, u32[]{:S(2)}) copy-start(bf16[384,128]{1,0:T(8,128)(2,1)S(1)} %convolution_convert_fusion.zx) | copy-start | bytes 294916
  177.5 24.2 %copy-start.1 = (f32[48,64,128]{2,1,0:T(8,128)S(1)}, f32[48,64,128]{2,1,0:T(8,128)}, u32[]{:S(2)}) copy-start(f32[48,64,128]{2,1,0:T(8,128)} %get-tuple-element.34) | copy-start | bytes 4718596
  182.4 19.3 %copy-start.2 = (f32[48,64,128]{2,1,0:T(8,128)S(1)}, f32[48,64,128]{2,1,0:T(8,128)}, u32[]{:S(2)}) copy-start(f32[48,64,128]{2,1,0:T(8,128)} %get-tuple-element.35) | copy-start | bytes 4718596
